TPU v7x, 32 devices: a whole 2x2x4 slice. The times are simulated.
32 devices in a mesh: grp: 2 (over x), freq: 16 (over z, y, core).
Axes of the slice: x: 2, y: 2, z: 4, core: 2. Of those that a mesh axis runs over, the one named last changes fastest.
Arguments:
- kernel: bfloat16 [2, 256, 1024, 1024], P(None, ('grp', 'freq')), parts along dimension 1, may hold values from -0.125 to 0.125
- recorded: float32 [2, 256, 1024, 128], P(None, ('grp', 'freq')), parts along dimension 1, may hold values from -8 to 8
- onset_time: int32 [2048, 128], P(('grp', 'freq')), parts along dimension 0, may hold values from 32 to 256, as said below
Outputs:
- focusing: float32 [256, 2048, 128], P(None, ('grp', 'freq')), parts along dimension 1
There are 2 independent parts, one for each index of `grp`. A program takes and returns all parts, laid end to end along the dimension named above; each array names one. Nothing has to cross between parts.
Inputs may be any that keep to these rules, and one draw needn't show every extreme that they name: `onset_time`: onset sample of the window for each receiver and focal point.
All inputs are finite; a program needn't handle non-finite values.
Results may differ from a plain program's by a relative error of at most 0.012.
Values may be sent and summed in bfloat16 or wider, within the bound.
A program may use at most 192 MiB of HBM per device.

v0:
```python
import math

import jax
import jax.numpy as jnp
from jax import lax
from jax.sharding import PartitionSpec as P

NF = 128
ITERS = 2


def dft_tables():
    samples = jnp.arange(2 * NF, dtype=jnp.int32)
    bins = jnp.arange(NF, dtype=jnp.int32)
    phase = (bins[:, None] * samples[None, :] % (2 * NF)).astype(jnp.float32) * (math.pi / NF)
    factor = 1.0 / math.sqrt(NF)
    return (jnp.cos(phase) * factor, jnp.sin(phase) * factor)


def square_sum(values):
    return jnp.sum(values * values)


def joint_total(first, second, third):
    return lax.psum((first, second, third), "freq")


def body(kernel, recorded, onset_time):
    highest = lax.Precision.HIGHEST
    cosine_table, sin_tab = dft_tables()
    rec_local = onset_time.shape[0]
    focal_count = onset_time.shape[1]
    samples = lax.broadcasted_iota(jnp.int32, (2 * NF, rec_local, focal_count), 0)
    keep_mask = (samples < onset_time[None]).astype(jnp.float32)
    kernel_real = kernel[0]
    kernel_imaginary = kernel[1]

    def invert(block_in):
        columns = block_in.shape[3]
        widened = block_in.astype(jnp.float32)
        timed = jnp.dot(cosine_table.T, widened[0].reshape(NF, -1), precision=highest) - jnp.dot(
            sin_tab.T, widened[1].reshape(NF, -1), precision=highest
        )
        return timed.reshape(2 * NF, block_in.shape[2], columns)

    def apply_adjoint(resid):
        rounded = resid.astype(jnp.bfloat16)
        update_real = rounded[0]
        update_imaginary = rounded[1]
        z_real = jnp.einsum(
            "hvi,hvg->hig", kernel_real, update_real, preferred_element_type=jnp.float32
        ) + jnp.einsum(
            "hvi,hvg->hig", kernel_imaginary, update_imaginary, preferred_element_type=jnp.float32
        )
        z_imag = jnp.einsum(
            "hvi,hvg->hig", kernel_real, update_imaginary, preferred_element_type=jnp.float32
        ) - jnp.einsum(
            "hvi,hvg->hig", kernel_imaginary, update_real, preferred_element_type=jnp.float32
        )
        image = jnp.stack([z_real, z_imag]).astype(jnp.bfloat16)
        timed = invert(lax.all_to_all(image, "freq", split_axis=2, concat_axis=1, tiled=True))
        return timed * keep_mask

    model_raw = apply_adjoint(recorded)
    totals = joint_total(square_sum(recorded), square_sum(model_raw), jnp.float32(0.0))
    beta_now = jnp.sqrt(totals[0])
    data_vec = recorded / beta_now
    alpha_now = jnp.sqrt(totals[1]) / beta_now
    model_vec = model_raw / (alpha_now * beta_now)
    search = model_vec
    estimate = jnp.zeros_like(model_vec)
    phibar_now = beta_now
    rhobar_now = alpha_now
    for iteration in range(ITERS):
        flat_part = (model_vec * keep_mask).reshape(2 * NF, -1)
        spec_real = jnp.dot(cosine_table, flat_part, precision=highest)
        spec_imag = -jnp.dot(sin_tab, flat_part, precision=highest)
        spectrum = (
            jnp.stack([spec_real, spec_imag])
            .reshape(2, NF, rec_local, focal_count)
            .astype(jnp.bfloat16)
        )
        multiply_block_in = lax.all_to_all(
            spectrum, "freq", split_axis=1, concat_axis=2, tiled=True
        )
        solution_real = multiply_block_in[0]
        solution_imaginary = multiply_block_in[1]
        y_real = jnp.einsum(
            "ptx,pxi->pti", kernel_real, solution_real, preferred_element_type=jnp.float32
        ) - jnp.einsum(
            "ptx,pxi->pti", kernel_imaginary, solution_imaginary, preferred_element_type=jnp.float32
        )
        y_imag = jnp.einsum(
            "ptx,pxi->pti", kernel_real, solution_imaginary, preferred_element_type=jnp.float32
        ) + jnp.einsum(
            "ptx,pxi->pti", kernel_imaginary, solution_real, preferred_element_type=jnp.float32
        )
        data_raw = jnp.stack([y_real, y_imag]) - alpha_now * data_vec
        image_raw = apply_adjoint(data_raw)
        totals = joint_total(
            square_sum(data_raw), square_sum(image_raw), jnp.sum(image_raw * model_vec)
        )
        beta_now = jnp.sqrt(totals[0])
        data_vec = data_raw / beta_now
        alpha_now = jnp.sqrt(
            totals[1] / (beta_now * beta_now) - 2.0 * totals[2] + beta_now * beta_now
        )
        model_vec = (image_raw / beta_now - beta_now * model_vec) / alpha_now
        rho_now = jnp.sqrt(rhobar_now * rhobar_now + beta_now * beta_now)
        cosine = rhobar_now / rho_now
        sine_part = beta_now / rho_now
        theta_now = sine_part * alpha_now
        rhobar_now = -cosine * alpha_now
        phi_now = cosine * phibar_now
        phibar_now = sine_part * phibar_now
        estimate = estimate + phi_now / rho_now * search
        search = model_vec - theta_now / rho_now * search
    return estimate


def solution(mesh):
    placed = (
        P(None, ("grp", "freq"), None, None),
        P(None, ("grp", "freq"), None, None),
        P(("grp", "freq"), None),
    )
    return jax.shard_map(
        body, mesh=mesh, in_specs=placed, out_specs=P(None, ("grp", "freq"), None), check_vma=False
    )
```

profile of v0, /device:TPU:0, one launch (start us, length us, event | category | flops | bytes accessed | tf_op | source)
XLA Modules:
  0.0 832.4 jit_solution(1631037788863570241)
XLA Ops:
  8.5 10.8 %fusion.14 = f32[8,1024,128]{2,1,0:T(8,128)} fusion(bf16[2,8,1024,1024]{3,2,1,0:T(8,128)(2,1)} %param.3, bf16[2,8,1024,128]{3,2,1,0:T(8,128)(2,1)S(1)} %get-tuple-element.15), kind=kOutput, calls=%fused_computation.14 | convolution fusion | flops 2147483648 | bytes 23068672 | tf_op jit(solution)/shard_map/hvi,hvg->hig/dot_general | solution.py:52
  19.4 10.7 %fusion.12 = f32[8,1024,128]{2,1,0:T(8,128)} fusion(bf16[2,8,1024,1024]{3,2,1,0:T(8,128)(2,1)} %param.3, bf16[2,8,1024,128]{3,2,1,0:T(8,128)(2,1)S(1)} %get-tuple-element.15), kind=kOutput, calls=%fused_computation.12 | convolution fusion | flops 2147483648 | bytes 23068672 | tf_op jit(solution)/shard_map/hvi,hvg->hig/dot_general | solution.py:57
  39.7 10.4 %fusion.68 = bf16[1,8,1024,128]{3,2,1,0:T(8,128)(2,1)S(1)} fusion(f32[8,1024,128]{2,1,0:T(8,128)} %fusion.12, bf16[2,8,1024,128]{3,2,1,0:T(8,128)(2,1)S(1)} %get-tuple-element.15, bf16[2,8,1024,1024]{3,2,1,0:T(8,128)(2,1)} %param.3), kind=kOutput, calls=%fused_computation.98 | convolution fusion | flops 2149580800 | bytes 25165824 | tf_op jit(solution)/shard_map/hvi,hvg->hig/dot_general | solution.py:55
  53.2 99.3 %all_to_all.60 = bf16[2,8,1024,128]{3,1,0,2:T(8,128)(2,1)S(1)} all-to-all(bf16[2,8,1024,128]{3,1,0,2:T(8,128)(2,1)S(1)} %copy.81), channel_id=1, replica_groups=mesh['grp'=2,'freq'=16] {'freq'}, dimensions={2} | all-to-all | bytes 8388608 | tf_op jit(solution)/shard_map/all_to_all | solution.py:61
  159.0 12.1 %multiply_reduce_fusion.4 = (f32[]{:T(128)}, f32[256,8192]{1,0:T(8,128)}) fusion(s32[8192]{0:T(1024)S(1)} %bitcast.250, f32[256,8192]{1,0:T(8,128)S(1)} %fusion.78, bf16[16,8,64,128]{3,2,1,0:T(8,128)(2,1)S(1)} %get-tuple-element.22), kind=kOutput, calls=%fused_computation.58 | convolution fusion | flops 3232202752 | bytes 18907140 | tf_op jit(solution)/shard_map/dot_general | solution.py:41
  171.1 34.1 %all-reduce.1 = (f32[]{:T(128)}, f32[]{:T(128)}) all-reduce(f32[]{:T(128)} %get-tuple-element.24, f32[]{:T(128)} %get-tuple-element.14), channel_id=1, replica_groups=mesh['grp'=2,'freq'=16] {'freq'}, use_global_device_ids=true, to_apply=%region_1.2 | all-reduce | flops 2 | bytes 16 | tf_op jit(solution)/shard_map/psum | solution.py:25
  206.5 10.7 %fusion.89 = bf16[16,8,64,128]{3,1,2,0:T(8,128)(2,1)S(1)} fusion(s32[8192]{0:T(1024)S(1)} %bitcast.251, f32[256,8192]{1,0:T(8,128)} %get-tuple-element.25, f32[]{:T(128)S(6)} %mul.210), kind=kOutput, calls=%fused_computation.123 | convolution fusion | flops 3231154176 | bytes 10518532 | tf_op jit(solution)/shard_map/dot_general | solution.py:76
  242.5 68.8 %all-to-all-done.1 = bf16[2,128,64,128]{3,2,0,1:T(8,128)(2,1)} async-done(((bf16[2,128,64,128]{3,2,0,1:T(8,128)(2,1)}), bf16[2,128,64,128]{3,2,0,1:T(8,128)(2,1)}, u32[]{:S(2)}, u32[]{:S(2)}) %all-to-all-start.1) | async-done | bytes 4194336 | tf_op jit(solution)/shard_map/all_to_all | solution.py:83
  316.9 14.0 %fusion.10 = f32[8,128,1024]{2,1,0:T(8,128)} fusion(bf16[8,1024,128]{2,1,0:T(8,128)(2,1)} %bitcast.241, bf16[2,8,1024,1024]{3,2,1,0:T(8,128)(2,1)} %param.3), kind=kOutput, calls=%fused_computation.10 | convolution fusion | flops 2147483648 | bytes 23068672 | tf_op jit(solution)/shard_map/ptx,pxi->pti/dot_general | solution.py:90
  332.5 14.0 %fusion.8 = f32[8,128,1024]{2,1,0:T(8,128)} fusion(bf16[8,1024,128]{2,1,0:T(8,128)(2,1)} %bitcast.246, bf16[2,8,1024,1024]{3,2,1,0:T(8,128)(2,1)} %param.3), kind=kOutput, calls=%fused_computation.8 | convolution fusion | flops 2147483648 | bytes 23068672 | tf_op jit(solution)/shard_map/ptx,pxi->pti/dot_general | solution.py:95
  346.5 10.8 %subtract_bitcast_fusion.1 = f32[1,8,1024,128]{2,3,1,0:T(8,128)S(1)} fusion(f32[8,128,1024]{2,1,0:T(8,128)} %fusion.10, bf16[8,1024,128]{2,1,0:T(8,128)(2,1)} %bitcast.247, bf16[2,8,1024,1024]{3,2,1,0:T(8,128)(2,1)} %param.3), kind=kOutput, calls=%fused_computation.74 | convolution fusion | flops 2148532224 | bytes 27262976 | tf_op jit(solution)/shard_map/ptx,pxi->pti/dot_general | solution.py:88
  357.3 11.2 %add_bitcast_fusion.1 = f32[1,8,1024,128]{2,3,1,0:T(8,128)} fusion(f32[8,128,1024]{2,1,0:T(8,128)} %fusion.8, bf16[8,1024,128]{2,1,0:T(8,128)(2,1)S(1)} %bitcast.242, bf16[2,8,1024,1024]{3,2,1,0:T(8,128)(2,1)} %param.3), kind=kOutput, calls=%fused_computation.73 | convolution fusion | flops 2148532224 | bytes 27262976 | tf_op jit(solution)/shard_map/ptx,pxi->pti/dot_general | solution.py:93
  378.8 10.1 %fusion.6 = f32[8,128,1024]{2,1,0:T(8,128)} fusion(bf16[2,8,1024,1024]{3,2,1,0:T(8,128)(2,1)} %param.3, bf16[2,8,1024,128]{2,3,1,0:T(8,128)(2,1)S(1)} %convert_element_type.32), kind=kOutput, calls=%fused_computation.6 | convolution fusion | flops 2147483648 | bytes 23068672 | tf_op jit(solution)/shard_map/hvi,hvg->hig/dot_general | solution.py:52
  388.9 10.1 %fusion.4 = f32[8,128,1024]{2,1,0:T(8,128)} fusion(bf16[2,8,1024,1024]{3,2,1,0:T(8,128)(2,1)} %param.3, bf16[2,8,1024,128]{2,3,1,0:T(8,128)(2,1)S(1)} %convert_element_type.32), kind=kOutput, calls=%fused_computation.4 | convolution fusion | flops 2147483648 | bytes 23068672 | tf_op jit(solution)/shard_map/hvi,hvg->hig/dot_general | solution.py:57
  408.5 10.8 %fusion.70 = bf16[1,8,1024,128]{2,3,1,0:T(8,128)(2,1)} fusion(f32[8,128,1024]{2,1,0:T(8,128)} %fusion.4, bf16[2,8,1024,1024]{3,2,1,0:T(8,128)(2,1)} %param.3, bf16[2,8,1024,128]{2,3,1,0:T(8,128)(2,1)S(1)} %convert_element_type.32), kind=kOutput, calls=%fused_computation.100 | convolution fusion | flops 2149580800 | bytes 25165824 | tf_op jit(solution)/shard_map/hvi,hvg->hig/dot_general | solution.py:55
  430.2 112.1 %all_to_all.61 = bf16[2,8,1024,128]{3,1,0,2:T(8,128)(2,1)S(1)} all-to-all(bf16[2,8,1024,128]{3,1,0,2:T(8,128)(2,1)} %copy.101), channel_id=1, replica_groups=mesh['grp'=2,'freq'=16] {'freq'}, dimensions={2} | all-to-all | bytes 8388608 | tf_op jit(solution)/shard_map/all_to_all | solution.py:61
  549.1 11.3 %multiply_reduce_fusion = (f32[]{:T(128)}, f32[]{:T(128)}, f32[256,8192]{1,0:T(8,128)}) fusion(s32[8192]{0:T(1024)S(1)} %bitcast.253, f32[]{:T(128)S(6)} %mul.210, f32[256,8192]{1,0:T(8,128)S(1)} %bitcast.229, f32[256,8192]{1,0:T(8,128)S(1)} %fusion.73, bf16[16,8,64,128]{3,2,1,0:T(8,128)(2,1)S(1)} %bitcast.245), kind=kOutput, calls=%fused_computation.53 | convolution fusion | flops 3240591360 | bytes 27295756 | tf_op jit(solution)/shard_map/dot_general | solution.py:41
  560.4 34.2 %all-reduce = (f32[]{:T(128)}, f32[]{:T(128)}, f32[]{:T(128)}) all-reduce(f32[]{:T(128)} %get-tuple-element.12, f32[]{:T(128)} %get-tuple-element.6, f32[]{:T(128)} %get-tuple-element.5), channel_id=1, replica_groups=mesh['grp'=2,'freq'=16] {'freq'}, use_global_device_ids=true, to_apply=%region_5.6 | all-reduce | flops 3 | bytes 24 | tf_op jit(solution)/shard_map/psum | solution.py:25
  632.4 68.8 %all-to-all-done.3 = bf16[2,128,64,128]{3,2,0,1:T(8,128)(2,1)} async-done(((bf16[2,128,64,128]{3,2,0,1:T(8,128)(2,1)}), bf16[2,128,64,128]{3,2,0,1:T(8,128)(2,1)}, u32[]{:S(2)}, u32[]{:S(2)}) %all-to-all-start.3) | async-done | bytes 4194336 | tf_op jit(solution)/shard_map/all_to_all | solution.py:83
  706.8 14.0 %fusion.2 = f32[8,128,1024]{2,1,0:T(8,128)} fusion(bf16[8,1024,128]{2,1,0:T(8,128)(2,1)} %bitcast.243, bf16[2,8,1024,1024]{3,2,1,0:T(8,128)(2,1)} %param.3), kind=kOutput, calls=%fused_computation.2 | convolution fusion | flops 2147483648 | bytes 23068672 | tf_op jit(solution)/shard_map/ptx,pxi->pti/dot_general | solution.py:90
  722.4 14.3 %fusion = f32[8,128,1024]{2,1,0:T(8,128)} fusion(bf16[8,1024,128]{2,1,0:T(8,128)(2,1)} %bitcast.248, bf16[2,8,1024,1024]{3,2,1,0:T(8,128)(2,1)} %param.3), kind=kOutput, calls=%fused_computation | convolution fusion | flops 2147483648 | bytes 23068672 | tf_op jit(solution)/shard_map/ptx,pxi->pti/dot_general | solution.py:95
  736.8 10.7 %subtract_bitcast_fusion = f32[1,8,1024,128]{2,3,1,0:T(8,128)S(1)} fusion(f32[8,128,1024]{2,1,0:T(8,128)} %fusion.2, bf16[8,1024,128]{2,1,0:T(8,128)(2,1)} %bitcast.249, bf16[2,8,1024,1024]{3,2,1,0:T(8,128)(2,1)} %param.3), kind=kOutput, calls=%fused_computation.70 | convolution fusion | flops 2148532224 | bytes 27262976 | tf_op jit(solution)/shard_map/ptx,pxi->pti/dot_general | solution.py:88
  747.4 11.2 %add_bitcast_fusion = f32[1,8,1024,128]{2,3,1,0:T(8,128)} fusion(f32[8,128,1024]{2,1,0:T(8,128)} %fusion, bf16[8,1024,128]{2,1,0:T(8,128)(2,1)S(1)} %bitcast.244, bf16[2,8,1024,1024]{3,2,1,0:T(8,128)(2,1)} %param.3), kind=kOutput, calls=%fused_computation.69 | convolution fusion | flops 2148532224 | bytes 27262976 | tf_op jit(solution)/shard_map/ptx,pxi->pti/dot_general | solution.py:93
  773.2 48.3 %psum.47 = f32[]{:T(128)} all-reduce(f32[]{:T(128)} %fusion.40), channel_id=1, replica_groups=mesh['grp'=2,'freq'=16] {'freq'}, use_global_device_ids=true, to_apply=%region_11.12 | all-reduce | flops 1 | bytes 8 | tf_op jit(solution)/shard_map/psum | solution.py:25
  (60 shorter events, 164.4 us)
Async XLA Ops:
  154.5 4.4 copy-start.4
  206.5 10.7 %copy-start = (f32[256,8192]{1,0:T(8,128)S(1)}, f32[256,8192]{1,0:T(8,128)}, u32[]{:S(2)}) copy-start(f32[256,8192]{1,0:T(8,128)} %get-tuple-element.25) | copy-start | bytes 25165828
  229.2 82.0 %all-to-all-start.1 = ((bf16[2,128,64,128]{3,2,0,1:T(8,128)(2,1)}), bf16[2,128,64,128]{3,2,0,1:T(8,128)(2,1)}, u32[]{:S(2)}, u32[]{:S(2)}) async-start(bf16[2,128,64,128]{3,2,0,1:T(8,128)(2,1)} %pad_maximum_fusion.1), calls=%async_computation.1 | async-start | bytes 8388608 | tf_op jit(solution)/shard_map/all_to_all | solution.py:83
  346.5 10.8 %copy-start.2 = (bf16[1,8,16,64,128]{4,3,2,1,0:T(8,128)(2,1)S(1)}, bf16[1,8,16,64,128]{4,3,2,1,0:T(8,128)(2,1)}, u32[]{:S(2)}) copy-start(bf16[1,8,16,64,128]{4,3,2,1,0:T(8,128)(2,1)} %copy.89) | copy-start | bytes 6291460
  374.9 3.2 copy-start.1
  543.4 5.7 slice-start
  544.6 4.5 slice-start.1
  619.1 82.0 %all-to-all-start.3 = ((bf16[2,128,64,128]{3,2,0,1:T(8,128)(2,1)}), bf16[2,128,64,128]{3,2,0,1:T(8,128)(2,1)}, u32[]{:S(2)}, u32[]{:S(2)}) async-start(bf16[2,128,64,128]{3,2,0,1:T(8,128)(2,1)} %pad_maximum_fusion.3), calls=%async_computation.3 | async-start | bytes 8388608 | tf_op jit(solution)/shard_map/all_to_all | solution.py:83
  736.7 10.7 %copy-start.3 = (bf16[1,8,16,64,128]{4,3,2,1,0:T(8,128)(2,1)S(1)}, bf16[1,8,16,64,128]{4,3,2,1,0:T(8,128)(2,1)}, u32[]{:S(2)}) copy-start(bf16[1,8,16,64,128]{4,3,2,1,0:T(8,128)(2,1)} %copy.111) | copy-start | bytes 6291460
where the time goes:
time: 836 us; the launch traced here: 832 us
  blocking collectives  328 us (39%)
  matrix products  244 us (29%)
  waiting for transfers between devices  138 us (17%)
  local copies, waits for them, and re-layouts  60.7 us (7%)
  other arithmetic  47.7 us (6%)
  starting transfers between devices  9.31 us (1%)
    all_to_all x2, blocking collectives, apply_adjoint(): lax.all_to_all(image, 'freq', split_axis=2, concat_axis=1, tiled=True)  211 us
    all_to_all x2, waiting for transfers between devices, body(): lax.all_to_all(spectrum, 'freq', split_axis=1, concat_axis=2, tiled=True)  138 us
    psum x3, blocking collectives, joint_total(): return lax.psum((first, second, third), 'freq')  117 us
    unnamed x22, local copies, waits for them, and re-layouts  31.8 us
    dot_general x2, matrix products, body(): jnp.einsum('ptx,pxi->pti', kernel_imaginary, solution_real, preferred_ele...  28.3 us
    dot_general x2, matrix products, body(): jnp.einsum('ptx,pxi->pti', kernel_imaginary, solution_imaginary, preferre...  28 us
    dot_general x2, matrix products, invert(): jnp.dot(sin_tab.T, widened[1].reshape(NF, -1), precision=highest)  23.4 us
    dot_general x2, matrix products, body(): jnp.einsum('ptx,pxi->pti', kernel_real, solution_imaginary, preferred_ele...  22.4 us
  transfers between devices with their start and end apart: 2, of which 2 were waited for; matrix products, arithmetic and copies ran while one was open for 2% of the time, Pallas kernels for 0%

commit v1 on v0

v1 whole, which is shorter than its diff:
```python
import math

import jax
import jax.numpy as jnp
from jax import lax
from jax.sharding import PartitionSpec as P

ITERS = 2
CHUNKS = 2


def dft_table(bins_total):
    samples = jnp.arange(2 * bins_total, dtype=jnp.int32)
    bins = jnp.arange(bins_total, dtype=jnp.int32)
    phase = (bins[:, None] * samples[None, :] % (2 * bins_total)).astype(jnp.float32) * (math.pi / bins_total)
    factor = 1.0 / math.sqrt(bins_total)
    return jnp.stack([jnp.cos(phase) * factor, -jnp.sin(phase) * factor])


def square_sum(values):
    return jnp.sum(values * values)


def make_body(mesh):
    members = mesh.shape["freq"]

    def joint(*values):
        row = jnp.zeros((128,), jnp.float32)
        for place, value in enumerate(values):
            row = row.at[place].set(value)
        spread = jnp.broadcast_to(row, (members, 128))
        got = lax.all_to_all(spread, "freq", split_axis=0, concat_axis=0, tiled=True)
        total = jnp.sum(got, axis=0)
        return [total[place] for place in range(len(values))]

    def body(kernel, recorded, onset_time):
        own_bins = kernel.shape[1]
        sources = kernel.shape[2]
        receivers = kernel.shape[3]
        rec_local, focal = onset_time.shape
        bins_total = own_bins * members
        times = 2 * bins_total
        part = own_bins // CHUNKS
        rows = 2 * part
        table = dft_table(bins_total).astype(jnp.bfloat16)
        table = table.reshape(2, members, CHUNKS, part, times)
        tables = [
            table[:, :, c].transpose(1, 0, 2, 3).reshape(members * rows, times) for c in range(CHUNKS)
        ]
        steps = lax.broadcasted_iota(jnp.int32, (rec_local, times, focal), 1)
        keep_mask = (steps < onset_time[:, None, :]).astype(jnp.float32)
        real = [kernel[0, c * part:(c + 1) * part] for c in range(CHUNKS)]
        imag = [kernel[1, c * part:(c + 1) * part] for c in range(CHUNKS)]

        def exchange(block):
            return lax.all_to_all(block, "freq", split_axis=0, concat_axis=0, tiled=True)

        def image_part(c, resid):
            low = resid.astype(jnp.bfloat16)
            turned = jnp.concatenate([low[..., focal:], -low[..., :focal]], axis=-1)
            z = jnp.einsum("hvi,hvg->hig", real[c], low, preferred_element_type=jnp.float32)
            z = z + jnp.einsum("hvi,hvg->hig", imag[c], turned, preferred_element_type=jnp.float32)
            z = z.astype(jnp.bfloat16).reshape(part, members, rec_local, 2, focal)
            z = z.transpose(1, 2, 3, 0, 4).reshape(members, rec_local, rows, focal)
            return exchange(z)

        def to_time(images):
            total = 0.0
            for c in range(CHUNKS):
                block = images[c].transpose(1, 0, 2, 3).reshape(rec_local, members * rows, focal)
                total = total + jnp.einsum(
                    "kt,rkq->rtq", tables[c], block, preferred_element_type=jnp.float32
                )
            return total * keep_mask

        def to_spectrum(field):
            low = field.astype(jnp.bfloat16)
            out = []
            for c in range(CHUNKS):
                spec = jnp.einsum("kt,rtq->rkq", tables[c], low, preferred_element_type=jnp.float32)
                spec = spec.astype(jnp.bfloat16).reshape(rec_local, members, rows, focal)
                out.append(exchange(spec.transpose(1, 0, 2, 3)))
            return out

        def forward_part(c, spec):
            spec = spec.reshape(receivers, 2, part, focal).transpose(2, 0, 1, 3)
            spec = spec.reshape(part, receivers, 2 * focal)
            turned = jnp.concatenate([-spec[..., focal:], spec[..., :focal]], axis=-1)
            y = jnp.einsum("hvi,hig->hvg", real[c], spec, preferred_element_type=jnp.float32)
            return y + jnp.einsum("hvi,hig->hvg", imag[c], turned, preferred_element_type=jnp.float32)

        data = []
        for c in range(CHUNKS):
            piece = recorded[:, c * part:(c + 1) * part]
            data.append(jnp.concatenate([piece[0], piece[1]], axis=-1))
        raw = to_time([image_part(c, data[c]) for c in range(CHUNKS)])
        sum_b, sum_z = joint(square_sum(recorded), square_sum(raw))
        beta = jnp.sqrt(sum_b)
        image_norm = jnp.sqrt(sum_z)
        alpha = image_norm / beta
        field, field_scale = raw, 1.0 / image_norm
        data_scale = 1.0 / beta
        phibar, rhobar = beta, alpha
        fields = [lax.optimization_barrier(raw.transpose(1, 0, 2))]
        search = [field_scale]
        estimate = [jnp.float32(0.0)]
        for iteration in range(ITERS):
            spectra = to_spectrum(field)
            fresh = []
            images = []
            data_squares = 0.0
            for c in range(CHUNKS):
                piece = forward_part(c, spectra[c]) * field_scale - (alpha * data_scale) * data[c]
                data_squares = data_squares + square_sum(piece)
                fresh.append(piece)
                if iteration + 1 < ITERS:
                    images.append(image_part(c, piece))
            (sum_u,) = joint(data_squares)
            beta = jnp.sqrt(sum_u)
            data, data_scale = fresh, 1.0 / beta
            rho = jnp.sqrt(rhobar * rhobar + beta * beta)
            cosine = rhobar / rho
            sine = beta / rho
            phi = cosine * phibar
            phibar = sine * phibar
            estimate = [e + phi / rho * s for e, s in zip(estimate, search)]
            if iteration + 1 == ITERS:
                break
            field = to_time(images) * data_scale - (beta * field_scale) * field
            (sum_v,) = joint(square_sum(field))
            alpha = jnp.sqrt(sum_v)
            field_scale = 1.0 / alpha
            theta = sine * alpha
            rhobar = -cosine * alpha
            fields.append(lax.optimization_barrier(field.transpose(1, 0, 2)))
            search = [-(theta / rho) * s for s in search] + [field_scale]
            estimate = estimate + [jnp.float32(0.0)]
        total = 0.0
        for e, f in zip(estimate, fields):
            total = total + e * f
        return total

    return body


def solution(mesh):
    placed = (
        P(None, ("grp", "freq"), None, None),
        P(None, ("grp", "freq"), None, None),
        P(("grp", "freq"), None),
    )
    return jax.shard_map(
        make_body(mesh), mesh=mesh, in_specs=placed, out_specs=P(None, ("grp", "freq"), None), check_vma=False
    )
```

time: 836 us -> 685 us (0.82)
  blocking collectives: 328 us -> 0 us
  starting transfers between devices: 9.31 us -> 117 us
  waiting for transfers between devices: 138 us -> 224 us
  matrix products: 244 us -> 174 us
  local copies, waits for them, and re-layouts: 60.7 us -> 111 us
    all_to_all x2 -> x0, blocking collectives: 211 us -> none  [apply_adjoint(): lax.all_to_all(image, 'freq', split_axis=2, concat_axis=1, tiled=True)]
    psum x3 -> x0, blocking collectives: 117 us -> none  [joint_total(): return lax.psum((first, second, third), 'freq')]
    all_to_all x2 -> x12, starting transfers between devices: 9.31 us -> 117 us  [the longest x8 71.8 us: exchange(): lax.all_to_all(block, 'freq', split_axis=0, concat_axis=0, tiled=True)]
    all_to_all x2 -> x12, waiting for transfers between devices: 138 us -> 224 us  [the longest x8 217 us: exchange(): lax.all_to_all(block, 'freq', split_axis=0, concat_axis=0, tiled=True)]
    dot_general x24, matrix products: 244 us -> 174 us  [the longest x4 39.3 us: forward_part(): jnp.einsum('hvi,hig->hvg', real[c], spec, preferred_element_type=jnp.floa...]
    transpose x0 -> x10, local copies, waits for them, and re-layouts: none -> 29 us  [the longest x4 15 us: forward_part(): spec = spec.reshape(receivers, 2, part, focal).transpose(2, 0, 1, 3)]
    reshape x0 -> x10, local copies, waits for them, and re-layouts: none -> 24.8 us  [the longest x4 14 us: image_part(): z = z.astype(jnp.bfloat16).reshape(part, members, rec_local, 2, focal)]
    unnamed x22 -> x28, local copies, waits for them, and re-layouts: 31.8 us -> 10.9 us
  transfers between devices with their start and end apart: 2 -> 12, of which waited for: 2 -> 9; matrix products, arithmetic and copies ran while one was open for 2% -> 21% of each run, Pallas kernels for 0% -> 0%
where the time goes in v1:
time: 685 us; the launch traced here: 675 us
  waiting for transfers between devices  224 us (33%)
  matrix products  174 us (25%)
  starting transfers between devices  117 us (17%)
  local copies, waits for them, and re-layouts  111 us (16%)
  other arithmetic  43.5 us (6%)
    all_to_all x8, waiting for transfers between devices, exchange(): lax.all_to_all(block, 'freq', split_axis=0, concat_axis=0, tiled=True)  217 us
    all_to_all x8, starting transfers between devices, exchange(): lax.all_to_all(block, 'freq', split_axis=0, concat_axis=0, tiled=True)  71.8 us
    all_to_all x4, starting transfers between devices, joint(): lax.all_to_all(spread, 'freq', split_axis=0, concat_axis=0, tiled=True)  45 us
    dot_general x4, matrix products, forward_part(): jnp.einsum('hvi,hig->hvg', real[c], spec, preferred_element_type=jnp.floa...  39.3 us
    dot_general x4, matrix products, to_time(): jnp.einsum('kt,rkq->rtq', tables[c], block, preferred_element_type=jnp.fl...  39.1 us
    dot_general x4, matrix products, forward_part(): jnp.einsum('hvi,hig->hvg', imag[c], turned, preferred_element_type=jnp.fl...  31.3 us
    dot_general x4, matrix products, image_part(): jnp.einsum('hvi,hvg->hig', real[c], low, preferred_element_type=jnp.float32)  29.1 us
    dot_general x4, matrix products, image_part(): jnp.einsum('hvi,hvg->hig', imag[c], turned, preferred_element_type=jnp.fl...  19.3 us
  transfers between devices with their start and end apart: 12, of which 9 were waited for; matrix products, arithmetic and copies ran while one was open for 21% of the time, Pallas kernels for 0%

profile of v1, /device:TPU:0, one launch (start us, length us, event | category | flops | bytes accessed | tf_op | source)
XLA Modules:
  0.0 674.7 jit_solution(13697260572882564597)
XLA Ops:
  76.8 9.1 %all-to-all-done = bf16[16,64,8,128]{3,1,2,0:T(8,128)(2,1)} async-done(((bf16[16,64,8,128]{3,1,2,0:T(8,128)(2,1)}), bf16[16,64,8,128]{3,1,2,0:T(8,128)(2,1)}, u32[]{:S(2)}, u32[]{:S(2)}) %all-to-all-start) | async-done | bytes 2097184 | tf_op jit(solution)/shard_map/all_to_all | solution.py:56
  85.9 11.5 %all-to-all-start.1 = ((bf16[16,64,8,128]{3,1,2,0:T(8,128)(2,1)}), bf16[16,64,8,128]{3,1,2,0:T(8,128)(2,1)}, u32[]{:S(2)}, u32[]{:S(2)}) async-start(bf16[16,64,8,128]{3,1,2,0:T(8,128)(2,1)} %bitcast.228), calls=%async_computation.1 | async-start | bytes 4194304 | tf_op jit(solution)/shard_map/all_to_all | solution.py:56
  105.0 8.1 %fusion.92 = f32[64,128,256]{2,1,0:T(8,128)} fusion(bf16[128,256,1]{1,0,2:T(8,128)(2,1)S(1)} %reshape.332, bf16[64,128,128]{2,0,1:T(8,128)(2,1)} %bitcast.9), kind=kOutput, calls=%fused_computation.115 | convolution fusion | flops 536870912 | bytes 10551296 | tf_op jit(solution)/shard_map/kt,rkq->rtq/dot_general | solution.py:71
  113.1 25.3 %all-to-all-done.1 = bf16[16,64,8,128]{3,1,2,0:T(8,128)(2,1)} async-done(((bf16[16,64,8,128]{3,1,2,0:T(8,128)(2,1)}), bf16[16,64,8,128]{3,1,2,0:T(8,128)(2,1)}, u32[]{:S(2)}, u32[]{:S(2)}) %all-to-all-start.1) | async-done | bytes 2097184 | tf_op jit(solution)/shard_map/all_to_all | solution.py:56
  138.4 8.3 %multiply_reduce_fusion.1 = (f32[]{:T(128)}, f32[64,128,256]{2,1,0:T(8,128)}) fusion(s32[64,128]{1,0:T(8,128)S(1)} %copy-done.9, f32[64,128,256]{2,1,0:T(8,128)} %fusion.92, bf16[128,256,1]{1,0,2:T(8,128)(2,1)S(1)} %reshape.333, bf16[64,128,128]{2,0,1:T(8,128)(2,1)} %bitcast.20), kind=kOutput, calls=%fused_computation.43 | convolution fusion | flops 547356672 | bytes 18972676 | tf_op jit(solution)/shard_map/kt,rkq->rtq/dot_general | solution.py:71
  147.9 11.2 %all-to-all-start.2 = ((f32[16,1,128]{2,1,0:T(1,128)}), f32[16,1,128]{2,1,0:T(1,128)S(1)}, u32[]{:S(2)}, u32[]{:S(2)}) async-start(f32[16,1,128]{2,1,0:T(1,128)} %broadcast_in_dim.15), calls=%async_computation.2 | async-start | bytes 16384 | tf_op jit(solution)/shard_map/all_to_all | solution.py:32
  179.4 33.9 %all-to-all-done.4 = bf16[16,64,8,128]{3,1,2,0:T(8,128)(2,1)} async-done(((bf16[16,64,8,128]{3,1,2,0:T(8,128)(2,1)}), bf16[16,64,8,128]{3,1,2,0:T(8,128)(2,1)}, u32[]{:S(2)}, u32[]{:S(2)}) %all-to-all-start.4) | async-done | bytes 2097184 | tf_op jit(solution)/shard_map/all_to_all | solution.py:56
  213.3 11.7 %all-to-all-start.3 = ((bf16[16,64,8,128]{3,1,2,0:T(8,128)(2,1)}), bf16[16,64,8,128]{3,1,2,0:T(8,128)(2,1)}, u32[]{:S(2)}, u32[]{:S(2)}) async-start(bf16[16,64,8,128]{3,1,2,0:T(8,128)(2,1)} %bitcast.229), calls=%async_computation.3 | async-start | bytes 4194304 | tf_op jit(solution)/shard_map/all_to_all | solution.py:56
  236.9 29.1 %all-to-all-done.3 = bf16[16,64,8,128]{3,1,2,0:T(8,128)(2,1)} async-done(((bf16[16,64,8,128]{3,1,2,0:T(8,128)(2,1)}), bf16[16,64,8,128]{3,1,2,0:T(8,128)(2,1)}, u32[]{:S(2)}, u32[]{:S(2)}) %all-to-all-start.3) | async-done | bytes 2097184 | tf_op jit(solution)/shard_map/all_to_all | solution.py:56
  290.7 11.7 %fusion.141 = (bf16[4,1024,256]{1,2,0:T(8,128)(2,1)}, f32[]{:T(128)}, f32[4,1024,256]{1,2,0:T(8,128)}) fusion(f32[4,1024,128]{1,2,0:T(8,128)S(1)} %bitcast.226, f32[4,1024,128]{1,2,0:T(8,128)S(1)} %bitcast.224, f32[]{:T(128)S(6)} %mul.300, f32[]{:T(128)S(6)} %div.35, f32[4,256,1024]{2,1,0:T(8,128)} %fusion.8, bf16[4,1024,256]{1,2,0:T(8,128)(2,1)} %bitcast.231, ...), kind=kOutput, calls=%fused_computation.167 | convolution fusion | flops 2155872256 | bytes 25165836 | tf_op jit(solution)/shard_map/hvi,hig->hvg/dot_general | solution.py:89
  302.5 11.6 %fusion.142 = (bf16[4,1024,256]{1,2,0:T(8,128)(2,1)}, f32[]{:T(128)}, f32[4,1024,256]{1,2,0:T(8,128)}) fusion(f32[4,1024,128]{1,2,0:T(8,128)S(1)} %bitcast.222, f32[4,1024,128]{1,2,0:T(8,128)S(1)} %bitcast.220, f32[]{:T(128)S(6)} %mul.300, f32[]{:T(128)S(6)} %div.35, f32[4,256,1024]{2,1,0:T(8,128)} %fusion.24, bf16[4,1024,256]{1,2,0:T(8,128)(2,1)} %bitcast.234, ...), kind=kOutput, calls=%fused_computation.168 | convolution fusion | flops 2155872256 | bytes 25165836 | tf_op jit(solution)/shard_map/hvi,hig->hvg/dot_general | solution.py:89
  316.0 11.4 %all-to-all-start.5 = ((f32[16,1,128]{2,1,0:T(1,128)}), f32[16,1,128]{2,1,0:T(1,128)S(1)}, u32[]{:S(2)}, u32[]{:S(2)}) async-start(f32[16,1,128]{2,1,0:T(1,128)} %broadcast_in_dim.16), calls=%async_computation.5 | async-start | bytes 16384 | tf_op jit(solution)/shard_map/all_to_all | solution.py:32
  381.1 15.6 %all-to-all-done.7 = bf16[16,64,8,128]{3,1,2,0:T(8,128)(2,1)S(1)} async-done(((bf16[16,64,8,128]{3,1,2,0:T(8,128)(2,1)}), bf16[16,64,8,128]{3,1,2,0:T(8,128)(2,1)S(1)}, u32[]{:S(2)}, u32[]{:S(2)}) %all-to-all-start.7) | async-done | bytes 2097184 | tf_op jit(solution)/shard_map/all_to_all | solution.py:56
  396.7 11.5 %all-to-all-start.6 = ((bf16[16,64,8,128]{3,1,2,0:T(8,128)(2,1)}), bf16[16,64,8,128]{3,1,2,0:T(8,128)(2,1)}, u32[]{:S(2)}, u32[]{:S(2)}) async-start(bf16[16,64,8,128]{3,1,2,0:T(8,128)(2,1)} %bitcast.241), calls=%async_computation.6 | async-start | bytes 4194304 | tf_op jit(solution)/shard_map/all_to_all | solution.py:56
  414.7 34.5 %all-to-all-done.6 = bf16[16,64,8,128]{3,1,2,0:T(8,128)(2,1)} async-done(((bf16[16,64,8,128]{3,1,2,0:T(8,128)(2,1)}), bf16[16,64,8,128]{3,1,2,0:T(8,128)(2,1)}, u32[]{:S(2)}, u32[]{:S(2)}) %all-to-all-start.6) | async-done | bytes 2097184 | tf_op jit(solution)/shard_map/all_to_all | solution.py:56
  449.2 16.4 %bitcast_select_fusion.1 = (f32[256,64,128]{0,2,1:T(8,128)}, f32[256,64,128]{0,2,1:T(8,128)}, f32[64,128,256]{2,1,0:T(8,128)}) fusion(f32[64,128,256]{2,1,0:T(8,128)} %get-tuple-element.100, s32[64,128]{1,0:T(8,128)S(1)} %copy-done.9, f32[]{:T(128)S(6)} %mul.314, f32[]{:T(128)S(6)} %div.39, f32[64,128,256]{2,1,0:T(8,128)} %fusion.87, ...), kind=kOutput, calls=%fused_computation.3 | convolution fusion | flops 551550976 | bytes 44138504 | tf_op jit(solution)/shard_map/kt,rkq->rtq/dot_general | solution.py:71
  465.6 9.7 %multiply_reduce_fusion = (f32[]{:T(128)}, bf16[64,256,128]{1,2,0:T(8,128)(2,1)}) fusion(f32[64,128,256]{2,1,0:T(8,128)} %get-tuple-element.100, f32[]{:T(128)S(6)} %mul.314, f32[]{:T(128)S(6)} %div.39, f32[64,128,256]{2,1,0:T(8,128)} %get-tuple-element.103, f32[64,128,256]{2,1,0:T(8,128)S(1)} %copy-done, s32[64,128]{1,0:T(8,128)S(1)} %copy-done.9), kind=kLoop, calls=%fused_computation.42 | loop fusion | flops 20971520 | bytes 29392908 | tf_op jit(solution)/shard_map/reduce_sum | solution.py:21
  476.5 11.2 %all-to-all-start.8 = ((f32[16,1,128]{2,1,0:T(1,128)}), f32[16,1,128]{2,1,0:T(1,128)S(1)}, u32[]{:S(2)}, u32[]{:S(2)}) async-start(f32[16,1,128]{2,1,0:T(1,128)} %broadcast_in_dim.17), calls=%async_computation.8 | async-start | bytes 16384 | tf_op jit(solution)/shard_map/all_to_all | solution.py:32
  506.5 34.6 %all-to-all-done.10 = bf16[16,64,8,128]{3,1,2,0:T(8,128)(2,1)S(1)} async-done(((bf16[16,64,8,128]{3,1,2,0:T(8,128)(2,1)}), bf16[16,64,8,128]{3,1,2,0:T(8,128)(2,1)S(1)}, u32[]{:S(2)}, u32[]{:S(2)}) %all-to-all-start.10) | async-done | bytes 2097184 | tf_op jit(solution)/shard_map/all_to_all | solution.py:56
  541.1 11.5 %all-to-all-start.9 = ((bf16[16,64,8,128]{3,1,2,0:T(8,128)(2,1)}), bf16[16,64,8,128]{3,1,2,0:T(8,128)(2,1)}, u32[]{:S(2)}, u32[]{:S(2)}) async-start(bf16[16,64,8,128]{3,1,2,0:T(8,128)(2,1)} %bitcast.238), calls=%async_computation.9 | async-start | bytes 4194304 | tf_op jit(solution)/shard_map/all_to_all | solution.py:56
  558.5 35.2 %all-to-all-done.9 = bf16[16,64,8,128]{3,1,2,0:T(8,128)(2,1)} async-done(((bf16[16,64,8,128]{3,1,2,0:T(8,128)(2,1)}), bf16[16,64,8,128]{3,1,2,0:T(8,128)(2,1)}, u32[]{:S(2)}, u32[]{:S(2)}) %all-to-all-start.9) | async-done | bytes 2097184 | tf_op jit(solution)/shard_map/all_to_all | solution.py:56
  636.1 11.2 %all-to-all-start.11 = ((f32[16,1,128]{2,1,0:T(1,128)}), f32[16,1,128]{2,1,0:T(1,128)S(1)}, u32[]{:S(2)}, u32[]{:S(2)}) async-start(f32[16,1,128]{2,1,0:T(1,128)} %broadcast_in_dim.18), calls=%async_computation.11 | async-start | bytes 16384 | tf_op jit(solution)/shard_map/all_to_all | solution.py:32
  654.0 11.6 %multiply_add_fusion = f32[256,64,128]{0,2,1:T(8,128)} fusion(f32[256,64,128]{0,2,1:T(8,128)} %get-tuple-element.68, f32[256,64,128]{0,2,1:T(8,128)} %get-tuple-element.67, f32[]{:T(128)S(6)} %mul.341, f32[]{:T(128)S(6)} %add.131), kind=kLoop, calls=%fused_computation.40 | loop fusion | flops 6291456 | bytes 25165832 | tf_op jit(solution)/shard_map/add | solution.py:140
  665.6 8.7 %copy.244 = f32[256,64,128]{2,1,0:T(8,128)} copy(f32[256,64,128]{0,2,1:T(8,128)} %multiply_add_fusion) | data formatting | bytes 16777216 | tf_op jit(solution)/shard_map/add | solution.py:140
  (112 shorter events, 274.5 us)
Async XLA Ops:
  37.4 48.5 %all-to-all-start = ((bf16[16,64,8,128]{3,1,2,0:T(8,128)(2,1)}), bf16[16,64,8,128]{3,1,2,0:T(8,128)(2,1)}, u32[]{:S(2)}, u32[]{:S(2)}) async-start(bf16[16,64,8,128]{3,1,2,0:T(8,128)(2,1)} %bitcast.232), calls=%async_computation | async-start | bytes 4194304 | tf_op jit(solution)/shard_map/all_to_all | solution.py:56
  85.9 52.5 %all-to-all-start.1 = ((bf16[16,64,8,128]{3,1,2,0:T(8,128)(2,1)}), bf16[16,64,8,128]{3,1,2,0:T(8,128)(2,1)}, u32[]{:S(2)}, u32[]{:S(2)}) async-start(bf16[16,64,8,128]{3,1,2,0:T(8,128)(2,1)} %bitcast.228), calls=%async_computation.1 | async-start | bytes 4194304 | tf_op jit(solution)/shard_map/all_to_all | solution.py:56
  104.9 33.4 %copy-start.9 = (s32[64,128]{1,0:T(8,128)S(1)}, s32[64,128]{1,0:T(8,128)}, u32[]{:S(2)}) copy-start(s32[64,128]{1,0:T(8,128)} %param.15) | copy-start | bytes 98308
  147.9 18.3 %all-to-all-start.2 = ((f32[16,1,128]{2,1,0:T(1,128)}), f32[16,1,128]{2,1,0:T(1,128)S(1)}, u32[]{:S(2)}, u32[]{:S(2)}) async-start(f32[16,1,128]{2,1,0:T(1,128)} %broadcast_in_dim.15), calls=%async_computation.2 | async-start | bytes 16384 | tf_op jit(solution)/shard_map/all_to_all | solution.py:32
  166.2 47.1 %all-to-all-start.4 = ((bf16[16,64,8,128]{3,1,2,0:T(8,128)(2,1)}), bf16[16,64,8,128]{3,1,2,0:T(8,128)(2,1)}, u32[]{:S(2)}, u32[]{:S(2)}) async-start(bf16[16,64,8,128]{3,1,2,0:T(8,128)(2,1)} %bitcast.243), calls=%async_computation.4 | async-start | bytes 4194304 | tf_op jit(solution)/shard_map/all_to_all | solution.py:56
  213.3 52.7 %all-to-all-start.3 = ((bf16[16,64,8,128]{3,1,2,0:T(8,128)(2,1)}), bf16[16,64,8,128]{3,1,2,0:T(8,128)(2,1)}, u32[]{:S(2)}, u32[]{:S(2)}) async-start(bf16[16,64,8,128]{3,1,2,0:T(8,128)(2,1)} %bitcast.229), calls=%async_computation.3 | async-start | bytes 4194304 | tf_op jit(solution)/shard_map/all_to_all | solution.py:56
  273.1 1.9 copy-start.7
  282.7 8.0 %copy-start.2 = (f32[1,4,1024,128]{2,3,1,0:T(8,128)S(1)}, f32[1,4,1024,128]{2,3,1,0:T(8,128)}, u32[]{:S(2)}) copy-start(f32[1,4,1024,128]{2,3,1,0:T(8,128)} %copy.267) | copy-start | bytes 6291460
  282.7 8.0 %copy-start.3 = (f32[1,4,1024,128]{2,3,1,0:T(8,128)S(1)}, f32[1,4,1024,128]{2,3,1,0:T(8,128)}, u32[]{:S(2)}) copy-start(f32[1,4,1024,128]{2,3,1,0:T(8,128)} %copy.268) | copy-start | bytes 6291460
  290.7 11.8 %copy-start.1 = (f32[1,4,1024,128]{2,3,1,0:T(8,128)S(1)}, f32[1,4,1024,128]{2,3,1,0:T(8,128)}, u32[]{:S(2)}) copy-start(f32[1,4,1024,128]{2,3,1,0:T(8,128)} %copy.266) | copy-start | bytes 6291460
  316.0 33.6 %all-to-all-start.5 = ((f32[16,1,128]{2,1,0:T(1,128)}), f32[16,1,128]{2,1,0:T(1,128)S(1)}, u32[]{:S(2)}, u32[]{:S(2)}) async-start(f32[16,1,128]{2,1,0:T(1,128)} %broadcast_in_dim.16), calls=%async_computation.5 | async-start | bytes 16384 | tf_op jit(solution)/shard_map/all_to_all | solution.py:32
  329.1 4.9 copy-start.6
  349.6 47.1 %all-to-all-start.7 = ((bf16[16,64,8,128]{3,1,2,0:T(8,128)(2,1)}), bf16[16,64,8,128]{3,1,2,0:T(8,128)(2,1)S(1)}, u32[]{:S(2)}, u32[]{:S(2)}) async-start(bf16[16,64,8,128]{3,1,2,0:T(8,128)(2,1)} %bitcast.235), calls=%async_computation.7 | async-start | bytes 4194304 | tf_op jit(solution)/shard_map/all_to_all | solution.py:56
  357.4 4.9 copy-start.5
  396.7 52.5 %all-to-all-start.6 = ((bf16[16,64,8,128]{3,1,2,0:T(8,128)(2,1)}), bf16[16,64,8,128]{3,1,2,0:T(8,128)(2,1)}, u32[]{:S(2)}, u32[]{:S(2)}) async-start(bf16[16,64,8,128]{3,1,2,0:T(8,128)(2,1)} %bitcast.241), calls=%async_computation.6 | async-start | bytes 4194304 | tf_op jit(solution)/shard_map/all_to_all | solution.py:56
  449.2 16.4 %copy-start = (f32[64,128,256]{2,1,0:T(8,128)S(1)}, f32[64,128,256]{2,1,0:T(8,128)}, u32[]{:S(2)}) copy-start(f32[64,128,256]{2,1,0:T(8,128)} %fusion.87) | copy-start | bytes 25165828
  476.5 17.6 %all-to-all-start.8 = ((f32[16,1,128]{2,1,0:T(1,128)}), f32[16,1,128]{2,1,0:T(1,128)S(1)}, u32[]{:S(2)}, u32[]{:S(2)}) async-start(f32[16,1,128]{2,1,0:T(1,128)} %broadcast_in_dim.17), calls=%async_computation.8 | async-start | bytes 16384 | tf_op jit(solution)/shard_map/all_to_all | solution.py:32
  494.1 47.0 %all-to-all-start.10 = ((bf16[16,64,8,128]{3,1,2,0:T(8,128)(2,1)}), bf16[16,64,8,128]{3,1,2,0:T(8,128)(2,1)S(1)}, u32[]{:S(2)}, u32[]{:S(2)}) async-start(bf16[16,64,8,128]{3,1,2,0:T(8,128)(2,1)} %bitcast.242), calls=%async_computation.10 | async-start | bytes 4194304 | tf_op jit(solution)/shard_map/all_to_all | solution.py:56
  541.1 52.5 %all-to-all-start.9 = ((bf16[16,64,8,128]{3,1,2,0:T(8,128)(2,1)}), bf16[16,64,8,128]{3,1,2,0:T(8,128)(2,1)}, u32[]{:S(2)}, u32[]{:S(2)}) async-start(bf16[16,64,8,128]{3,1,2,0:T(8,128)(2,1)} %bitcast.238), calls=%async_computation.9 | async-start | bytes 4194304 | tf_op jit(solution)/shard_map/all_to_all | solution.py:56
  600.8 1.9 copy-start.8
  610.3 7.9 %copy-start.10 = (f32[4,1024,256]{1,2,0:T(8,128)S(1)}, f32[4,1024,256]{1,2,0:T(8,128)}, u32[]{:S(2)}) copy-start(f32[4,1024,256]{1,2,0:T(8,128)} %get-tuple-element.102) | copy-start | bytes 12582916
  618.3 8.1 %copy-start.4 = (bf16[4,1024,2,128]{1,3,2,0:T(8,128)(2,1)S(1)}, bf16[4,1024,2,128]{1,3,2,0:T(8,128)(2,1)}, u32[]{:S(2)}) copy-start(bf16[4,1024,2,128]{1,3,2,0:T(8,128)(2,1)} %copy.238) | copy-start | bytes 6291460
  618.3 8.1 %copy-start.11 = (f32[4,1024,256]{1,2,0:T(8,128)S(1)}, f32[4,1024,256]{1,2,0:T(8,128)}, u32[]{:S(2)}) copy-start(f32[4,1024,256]{1,2,0:T(8,128)} %get-tuple-element.101) | copy-start | bytes 12582916
  636.1 17.6 %all-to-all-start.11 = ((f32[16,1,128]{2,1,0:T(1,128)}), f32[16,1,128]{2,1,0:T(1,128)S(1)}, u32[]{:S(2)}, u32[]{:S(2)}) async-start(f32[16,1,128]{2,1,0:T(1,128)} %broadcast_in_dim.18), calls=%async_computation.11 | async-start | bytes 16384 | tf_op jit(solution)/shard_map/all_to_all | solution.py:32
